TPU v7x, 32 devices: a whole 2x2x4 slice. The times are simulated.
32 devices in a mesh: bank: 8 (over y, x, core), zero: 4 (over z).
Axes of the slice: x: 2, y: 2, z: 4, core: 2. Of those that a mesh axis runs over, the one named last changes fastest.
Arguments:
- master_down: float32 [64, 1024, 2048], P('bank', None, 'zero'), may hold values from -0.25 to 0.25
- router_weight: float32 [2048, 64], P('zero', 'bank'), may hold values from -0.125 to 0.125
- router_gain: float32 [2048], P('zero'), may hold values from 0.25 to 1.75
Outputs:
- final_down: bfloat16 [64, 1024, 2048], P('bank')
- scale_down: float32 [64, 1024], P('bank')
- serve_router: bfloat16 [2048, 64], replicated
All inputs are finite; a program needn't handle non-finite values. Where the computation divides by a largest or mean magnitude, that divisor is 1e-20 or more.
Results may differ from a plain program's by a relative error of at most 0.001.
Values may be sent and summed in bfloat16 or wider, within the bound.
A program may use at most 128 MiB of HBM per device.

v0:
```python
import jax
import jax.numpy as jnp
from jax import lax
from jax.sharding import PartitionSpec as P


def per_device(master_down, router_weight, router_gain):
    scale_down = lax.pmax(jnp.max(jnp.abs(master_down), axis=2), "zero")
    narrow_down = (master_down / jnp.expand_dims(scale_down, 2)).astype(jnp.bfloat16)
    final_down = lax.all_gather(narrow_down, "zero", axis=2, tiled=True)
    part_router = (router_weight * router_gain[:, None]).astype(jnp.bfloat16)
    row_router = lax.all_gather(part_router, "zero", axis=0, tiled=True)
    serve_router = lax.all_gather(row_router, "bank", axis=1, tiled=True)
    return (final_down, scale_down, serve_router)


def solution(mesh):
    placed = (P("bank", None, "zero"), P("zero", "bank"), P("zero"))
    return jax.shard_map(
        per_device,
        mesh=mesh,
        in_specs=placed,
        out_specs=(P("bank", None, None), P("bank", None), P()),
        check_vma=False,
    )
```

profile of v0, /device:TPU:0, one launch (start us, length us, event | category | flops | bytes accessed | tf_op | source)
XLA Modules:
  0.0 634.6 jit_solution(17249483322936477532)
XLA Ops:
  7.2 0.0 all-gather.2.cloned.1.call-start
  7.2 7.1 %abs_reduce_fusion = f32[8,1024]{1,0:T(8,128)S(1)} fusion(f32[8,1024,512]{2,1,0:T(8,128)} %param.3), kind=kLoop, calls=%fused_computation.1 | loop fusion | flops 8380416 | bytes 16809984 | tf_op jit(solution)/shard_map/reduce_max | solution.py:8
  14.3 20.8 %pmax.7 = f32[8,1024]{1,0:T(8,128)S(1)} all-reduce(f32[8,1024]{1,0:T(8,128)S(1)} %abs_reduce_fusion), channel_id=1, replica_groups=mesh['bank'=8,'zero'=4] {'zero'}, use_global_device_ids=true, to_apply=%region_1.0 | all-reduce | flops 8192 | bytes 65536 | tf_op jit(solution)/shard_map/pmax | solution.py:8
  35.1 0.0 copy-start
  35.1 0.0 copy-start.1
  35.2 0.0 copy-start.2
  35.2 9.2 %divide_convert_fusion = bf16[8,1024,512]{2,1,0:T(8,128)(2,1)} fusion(f32[8,1024,512]{2,1,0:T(8,128)} %param.3, f32[8,1024]{1,0:T(8,128)S(1)} %pmax.7), kind=kLoop, calls=%fused_computation | loop fusion | flops 8388608 | bytes 25198592 | tf_op jit(solution)/shard_map/convert_element_type | solution.py:9
  44.3 0.0 all-gather.2.cloned.1.call-update
  44.4 0.0 copy-done
  44.4 0.0 copy-done.1
  44.4 0.0 copy-done.2
  44.4 13.1 %all_gather.10 = bf16[2048,8]{0,1:T(8,128)(2,1)S(1)} all-gather(bf16[512,8]{0,1:T(8,128)(2,1)S(1)} %multiply_convert_fusion), channel_id=1, replica_groups=mesh['bank'=8,'zero'=4] {'zero'}, dimensions={0}, use_global_device_ids=true | all-gather | bytes 40960 | tf_op jit(solution)/shard_map/all_gather | solution.py:12
  57.5 9.3 %all_gather.11 = bf16[2048,64]{0,1:T(8,128)(2,1)S(1)} all-gather(bf16[2048,8]{0,1:T(8,128)(2,1)S(1)} %all_gather.10), channel_id=1, replica_groups=mesh['bank'=8,'zero'=4] {'bank'}, dimensions={1}, use_global_device_ids=true | all-gather | bytes 294912 | tf_op jit(solution)/shard_map/all_gather | solution.py:13
  66.8 537.3 %all-gather.2.cloned.1.call-done = bf16[8,1024,2048]{2,1,0:T(8,128)(2,1)} async-done(((bf16[8,1024,512]{2,1,0:T(8,128)(2,1)}), bf16[8,1024,2048]{2,1,0:T(8,128)(2,1)}) %all-gather.2.cloned.1.call-update) | async-done | bytes 33554448 | tf_op jit(solution)/shard_map/all_gather | solution.py:10
  604.1 22.9 %copy.8 = bf16[8,1024,2048]{2,1,0:T(8,128)(2,1)} copy(bf16[8,1024,2048]{2,1,0:T(8,128)(2,1)} %all-gather.2.cloned.1.call-done) | data formatting | bytes 67108864
  627.0 0.7 copy.9
  (1 shorter events, 0.0 us)
Async XLA Ops:
  7.2 597.0 %all-gather.2.cloned.1.call-start = ((), (), s32[]{:S(2)}) async-start(), calls=%async_computation | async-start | bytes 41943040 | tf_op jit(solution)/shard_map/all_gather | solution.py:10
  35.1 9.2 %copy-start = (f32[8,1024]{1,0:T(8,128)}, f32[8,1024]{1,0:T(8,128)S(1)}, u32[]{:S(2)}) copy-start(f32[8,1024]{1,0:T(8,128)S(1)} %pmax.7) | copy-start | bytes 98308
  35.1 9.2 %copy-start.1 = (f32[512,8]{0,1:T(8,128)S(1)}, f32[512,8]{0,1:T(8,128)}, u32[]{:S(2)}) copy-start(f32[512,8]{0,1:T(8,128)} %param.4) | copy-start | bytes 49156
  35.2 9.2 %copy-start.2 = (f32[512]{0:T(512)S(1)}, f32[512]{0:T(512)}, u32[]{:S(2)}) copy-start(f32[512]{0:T(512)} %param.5) | copy-start | bytes 6148
Sparse Core Ops, SparseCore 0:
  44.5 559.6 all-gather.1
where the time goes:
time: 635 us
  waiting for transfers between devices  537 us (85%)
  blocking collectives  43.2 us (7%)
  local copies, waits for them, and re-layouts  23.6 us (4%)
  other arithmetic  16.3 us (3%)
  between operations  14.1 us (2%)
    all_gather x1, waiting for transfers between devices, per_device(): final_down = lax.all_gather(narrow_down, 'zero', axis=2, tiled=True)  537 us
    unnamed x8, local copies, waits for them, and re-layouts  23.6 us
    pmax x1, blocking collectives, per_device(): scale_down = lax.pmax(jnp.max(jnp.abs(master_down), axis=2), 'zero')  20.8 us
    all_gather x1, blocking collectives, per_device(): row_router = lax.all_gather(part_router, 'zero', axis=0, tiled=True)  13.1 us
  transfers between devices with their start and end apart: 1, of which 1 were waited for; matrix products, arithmetic and copies ran while one was open for 0% of the time, Pallas kernels for 0%

commit v1 on v0

--- a/solution.py
+++ b/solution.py
@@ -7,7 +7,7 @@
 def per_device(master_down, router_weight, router_gain):
     scale_down = lax.pmax(jnp.max(jnp.abs(master_down), axis=2), "zero")
     narrow_down = (master_down / jnp.expand_dims(scale_down, 2)).astype(jnp.bfloat16)
-    final_down = lax.all_gather(narrow_down, "zero", axis=2, tiled=True)
+    final_down = jnp.concatenate(lax.all_gather(narrow_down, "zero"), axis=2)
     part_router = (router_weight * router_gain[:, None]).astype(jnp.bfloat16)
     row_router = lax.all_gather(part_router, "zero", axis=0, tiled=True)
     serve_router = lax.all_gather(row_router, "bank", axis=1, tiled=True)

time: 635 us -> 635 us (level)
    unnamed x8 -> x7, local copies, waits for them, and re-layouts: 23.6 us -> 0.72 us
    reshape x0 -> x1, local copies, waits for them, and re-layouts: none -> 22.8 us  [per_device(): final_down = jnp.concatenate(lax.all_gather(narrow_down, 'zero'), axis=2)]
where the time goes in v1:
time: 635 us
  waiting for transfers between devices  537 us (85%)
  blocking collectives  43.2 us (7%)
  local copies, waits for them, and re-layouts  23.5 us (4%)
  other arithmetic  16.3 us (3%)
  between operations  14.1 us (2%)
    all_gather x1, waiting for transfers between devices, per_device(): final_down = jnp.concatenate(lax.all_gather(narrow_down, 'zero'), axis=2)  537 us
    reshape x1, local copies, waits for them, and re-layouts, per_device(): final_down = jnp.concatenate(lax.all_gather(narrow_down, 'zero'), axis=2)  22.8 us
    pmax x1, blocking collectives, per_device(): scale_down = lax.pmax(jnp.max(jnp.abs(master_down), axis=2), 'zero')  20.8 us
    all_gather x1, blocking collectives, per_device(): row_router = lax.all_gather(part_router, 'zero', axis=0, tiled=True)  13.1 us
  transfers between devices with their start and end apart: 1, of which 1 were waited for; matrix products, arithmetic and copies ran while one was open for 0% of the time, Pallas kernels for 0%

profile of v1, /device:TPU:0, one launch (start us, length us, event | category | flops | bytes accessed | tf_op | source)
XLA Modules:
  0.0 634.5 jit_solution(10776684073163324914)
XLA Ops:
  7.2 0.0 all-gather.3.cloned.1.call-start
  7.2 7.1 %abs_reduce_fusion = f32[8,1024]{1,0:T(8,128)S(1)} fusion(f32[8,1024,512]{2,1,0:T(8,128)} %param.3), kind=kLoop, calls=%fused_computation.1 | loop fusion | flops 8380416 | bytes 16809984 | tf_op jit(solution)/shard_map/reduce_max | solution.py:8
  14.3 20.8 %pmax.7 = f32[8,1024]{1,0:T(8,128)S(1)} all-reduce(f32[8,1024]{1,0:T(8,128)S(1)} %abs_reduce_fusion), channel_id=1, replica_groups=mesh['bank'=8,'zero'=4] {'zero'}, use_global_device_ids=true, to_apply=%region_1.0 | all-reduce | flops 8192 | bytes 65536 | tf_op jit(solution)/shard_map/pmax | solution.py:8
  35.1 0.0 copy-start
  35.1 0.0 copy-start.1
  35.2 0.0 copy-start.2
  35.2 9.2 %divide_convert_fusion = bf16[8,1024,512]{2,1,0:T(8,128)(2,1)} fusion(f32[8,1024,512]{2,1,0:T(8,128)} %param.3, f32[8,1024]{1,0:T(8,128)S(1)} %pmax.7), kind=kLoop, calls=%fused_computation | loop fusion | flops 8388608 | bytes 25198592 | tf_op jit(solution)/shard_map/convert_element_type | solution.py:9
  44.3 0.0 all-gather.3.cloned.1.call-update
  44.4 0.0 copy-done
  44.4 0.0 copy-done.1
  44.4 0.0 copy-done.2
  44.4 13.1 %all_gather.14 = bf16[2048,8]{0,1:T(8,128)(2,1)S(1)} all-gather(bf16[512,8]{0,1:T(8,128)(2,1)S(1)} %multiply_convert_fusion), channel_id=1, replica_groups=mesh['bank'=8,'zero'=4] {'zero'}, dimensions={0}, use_global_device_ids=true | all-gather | bytes 40960 | tf_op jit(solution)/shard_map/all_gather | solution.py:12
  57.5 9.3 %all_gather.15 = bf16[2048,64]{0,1:T(8,128)(2,1)S(1)} all-gather(bf16[2048,8]{0,1:T(8,128)(2,1)S(1)} %all_gather.14), channel_id=1, replica_groups=mesh['bank'=8,'zero'=4] {'bank'}, dimensions={1}, use_global_device_ids=true | all-gather | bytes 294912 | tf_op jit(solution)/shard_map/all_gather | solution.py:13
  66.8 537.3 %all-gather.3.cloned.1.call-done = bf16[32,1024,512]{2,1,0:T(8,128)(2,1)} async-done(((bf16[8,1024,512]{2,1,0:T(8,128)(2,1)}), bf16[32,1024,512]{2,1,0:T(8,128)(2,1)}) %all-gather.3.cloned.1.call-update) | async-done | bytes 33554448 | tf_op jit(solution)/shard_map/all_gather | solution.py:10
  604.1 22.8 %copy.8 = bf16[4,8,128,8,512]{4,3,0,2,1:T(8,128)(2,1)} copy(bf16[4,8,128,8,512]{4,3,2,1,0:T(8,128)(2,1)} %bitcast.5) | data formatting | bytes 67108864 | tf_op jit(solution)/shard_map/reshape | solution.py:10
  627.0 0.7 copy.10
  (1 shorter events, 0.0 us)
Async XLA Ops:
  7.2 597.0 %all-gather.3.cloned.1.call-start = ((), (), s32[]{:S(2)}) async-start(), calls=%async_computation | async-start | bytes 41943040 | tf_op jit(solution)/shard_map/all_gather | solution.py:10
  35.1 9.2 %copy-start = (f32[8,1024]{1,0:T(8,128)}, f32[8,1024]{1,0:T(8,128)S(1)}, u32[]{:S(2)}) copy-start(f32[8,1024]{1,0:T(8,128)S(1)} %pmax.7) | copy-start | bytes 98308
  35.1 9.2 %copy-start.1 = (f32[512,8]{0,1:T(8,128)S(1)}, f32[512,8]{0,1:T(8,128)}, u32[]{:S(2)}) copy-start(f32[512,8]{0,1:T(8,128)} %param.4) | copy-start | bytes 49156
  35.2 9.2 %copy-start.2 = (f32[512]{0:T(512)S(1)}, f32[512]{0:T(512)}, u32[]{:S(2)}) copy-start(f32[512]{0:T(512)} %param.5) | copy-start | bytes 6148
Sparse Core Ops, SparseCore 0:
  44.5 559.6 all-gather.2
